TPU v7x, 32 devices: a whole 2x2x4 slice. The times are simulated.
32 devices in a mesh: grp: 4 (over z), row: 8 (over y, x, core).
Axes of the slice: x: 2, y: 2, z: 4, core: 2. Of those that a mesh axis runs over, the one named last changes fastest.
Arguments:
- expert_grams: float32 [4, 4096, 4096], P(None, 'row'), may hold values from -32 to 48, as said below
- expert_weights: bfloat16 [4, 4096, 512], P(None, 'row', 'grp'), may hold values from -6 to 6
Outputs:
- merged: float32 [4096, 512], P('row', 'grp')
- residual_ratio: float32 [], replicated
Inputs may be any that keep to these rules, and one draw needn't show every extreme that they name: Each expert_grams[k] is exactly symmetric and positive definite.
All inputs are finite; a program needn't handle non-finite values.
Results may differ from a plain program's by a relative error of at most 0.0003.
Values may be sent and summed in bfloat16 or wider, within the bound.
A program may use at most 128 MiB of HBM per device.

v0:
```python
import jax
import jax.numpy as jnp
from jax import lax
from jax.sharding import PartitionSpec as P

ITERS = 4


def both_sums(residual, mapped):
    return lax.psum(
        (jnp.sum(residual * residual, axis=0), jnp.sum(residual * mapped, axis=0)), "row"
    )


def local(expert_grams, expert_weights):
    rows_local = expert_grams.shape[1]
    full_width = expert_grams.shape[2]
    columns = expert_weights.shape[2]
    offset = lax.axis_index("row") * rows_local
    row_ids = offset + lax.broadcasted_iota(jnp.int32, (rows_local, full_width), 0)
    col_ids = lax.broadcasted_iota(jnp.int32, (rows_local, full_width), 1)
    system = jnp.sum(expert_grams, axis=0) + (row_ids == col_ids).astype(jnp.float32)
    empty = jnp.zeros((rows_local, columns), jnp.float32)
    target = jnp.einsum(
        "krn,knc->rc",
        expert_grams,
        lax.all_gather(expert_weights, "row", axis=1, tiled=True).astype(jnp.float32),
        precision=lax.Precision.HIGHEST,
        preferred_element_type=jnp.float32,
    )

    def add_panel(incoming):
        return jnp.dot(
            system, incoming, precision=lax.Precision.HIGHEST, preferred_element_type=jnp.float32
        )

    def apply_system(vectors):
        return add_panel(lax.all_gather(vectors, "row", axis=0, tiled=True))

    merged = empty
    residual = target
    mapped = apply_system(residual)
    norm_now, product = both_sums(residual, mapped)
    initial = norm_now
    step_size = norm_now / product
    direction = residual
    mapped_dir = mapped
    for iteration in range(ITERS):
        merged = merged + step_size * direction
        residual = residual - step_size * mapped_dir
        if iteration + 1 < ITERS:
            mapped = apply_system(residual)
            norm_next, product = both_sums(residual, mapped)
            scaling = norm_next / norm_now
            step_size = norm_next / (product - scaling * norm_next / step_size)
            direction = residual + scaling * direction
            mapped_dir = mapped + scaling * mapped_dir
            norm_now = norm_next
    final_sums = lax.psum(jnp.sum(residual * residual, axis=0), "row")
    totals = lax.psum((jnp.sum(final_sums), jnp.sum(initial)), "grp")
    residual_ratio = jnp.sqrt(totals[0] / totals[1])
    return (merged, residual_ratio)


def solution(mesh):
    placed = (P(None, "row", None), P(None, "row", "grp"))
    return jax.shard_map(
        local, mesh=mesh, in_specs=placed, out_specs=(P("row", "grp"), P()), check_vma=False
    )
```

profile of v0, /device:TPU:0, one launch (start us, length us, event | category | flops | bytes accessed | tf_op | source)
XLA Modules:
  0.0 311.2 jit_solution(3657418555997911050)
XLA Ops:
  7.2 0.0 all-gather.6.cloned.1.call-start
  7.2 0.7 all-gather.6.cloned.1.call-update
  7.9 0.0 all-gather.8.cloned.1.call-start
  7.9 41.3 %all-gather.6.cloned.1.call-done = bf16[4,4096,128]{2,1,0:T(8,128)(2,1)} async-done(((bf16[4,512,128]{2,1,0:T(8,128)(2,1)}), bf16[4,4096,128]{2,1,0:T(8,128)(2,1)}) %all-gather.6.cloned.1.call-update) | async-done | bytes 4194320 | tf_op jit(solution)/shard_map/all_gather | solution.py:27
  49.2 19.3 %convolution_bitcast_fusion = f32[512,128]{1,0:T(8,128)} fusion(f32[4,512,4096]{2,1,0:T(8,128)} %param.2, bf16[4,4096,128]{2,1,0:T(8,128)(2,1)} %all-gather.6.cloned.1.call-done), kind=kOutput, calls=%fused_computation.10 | convolution fusion | flops 12884901888 | bytes 38010880 | tf_op jit(solution)/shard_map/krn,knc->rc/dot_general | solution.py:24
  68.6 0.0 all-gather.8.cloned.1.call-update
  68.6 0.0 all-gather.10.cloned.1.call-start
  68.6 0.0 copy-start
  68.7 15.8 %reduce_sum.109 = f32[512,4096]{1,0:T(8,128)} reduce(f32[4,512,4096]{2,1,0:T(8,128)} %param.2, f32[]{:T(128)} %constant.3.clone.1), dimensions={0}, to_apply=%region_2.0 | reduce | flops 6291456 | bytes 41943044 | tf_op jit(solution)/shard_map/reduce_sum | solution.py:22
  84.5 12.0 %all-gather.8.cloned.1.call-done = f32[4096,128]{1,0:T(8,128)} async-done(((f32[512,128]{1,0:T(8,128)}), f32[4096,128]{1,0:T(8,128)}) %all-gather.8.cloned.1.call-update) | async-done | bytes 2097168 | tf_op jit(solution)/shard_map/all_gather | solution.py:38
  96.5 0.0 copy-done
  96.5 10.1 %multiply_reduce_fusion.7 = (f32[128]{0:T(128)S(1)}, f32[128]{0:T(128)S(1)}, f32[512,128]{1,0:T(8,128)S(1)}) fusion(f32[512,128]{1,0:T(8,128)S(1)} %copy-done, f32[4096,128]{1,0:T(8,128)} %all-gather.8.cloned.1.call-done, f32[512,4096]{1,0:T(8,128)} %reduce_sum.109, s32[512]{0:T(512)S(1)} %iota_add_fusion), kind=kOutput, calls=%fused_computation.24 | convolution fusion | flops 3227778816 | bytes 11013120 | tf_op jit(solution)/shard_map/dot_general | solution.py:33
  106.6 13.1 %all-reduce.3 = (f32[128]{0:T(128)S(1)}, f32[128]{0:T(128)S(1)}) all-reduce(f32[128]{0:T(128)S(1)} %get-tuple-element.9, f32[128]{0:T(128)S(1)} %get-tuple-element.8), channel_id=1, replica_groups=mesh['grp'=4,'row'=8] {'row'}, use_global_device_ids=true, to_apply=%region_1.0 | all-reduce | flops 256 | bytes 2048 | tf_op jit(solution)/shard_map/psum | solution.py:10
  119.7 0.7 multiply_subtract_fusion.2
  120.4 0.0 copy-start.2
  120.4 0.0 all-gather.10.cloned.1.call-update
  120.5 0.2 all-gather.12.cloned.1.call-start
  120.7 27.7 %all-gather.10.cloned.1.call-done = f32[4096,128]{1,0:T(8,128)} async-done(((f32[512,128]{1,0:T(8,128)}), f32[4096,128]{1,0:T(8,128)}) %all-gather.10.cloned.1.call-update) | async-done | bytes 2097168 | tf_op jit(solution)/shard_map/all_gather | solution.py:38
  148.4 10.1 %multiply_reduce_fusion.5 = (f32[128]{0:T(128)S(1)}, f32[128]{0:T(128)S(1)}, f32[512,128]{1,0:T(8,128)S(1)}) fusion(f32[512,128]{1,0:T(8,128)} %multiply_subtract_fusion.2, f32[4096,128]{1,0:T(8,128)} %all-gather.10.cloned.1.call-done, f32[512,4096]{1,0:T(8,128)} %reduce_sum.109, s32[512]{0:T(512)S(1)} %iota_add_fusion), kind=kOutput, calls=%fused_computation.21 | convolution fusion | flops 3227778816 | bytes 11013120 | tf_op jit(solution)/shard_map/dot_general | solution.py:33
  158.5 13.1 %all-reduce.2 = (f32[128]{0:T(128)S(1)}, f32[128]{0:T(128)S(1)}) all-reduce(f32[128]{0:T(128)S(1)} %get-tuple-element.7, f32[128]{0:T(128)S(1)} %get-tuple-element.6), channel_id=1, replica_groups=mesh['grp'=4,'row'=8] {'row'}, use_global_device_ids=true, to_apply=%region_6.0 | all-reduce | flops 256 | bytes 2048 | tf_op jit(solution)/shard_map/psum | solution.py:10
  171.6 0.6 fusion.9
  172.2 0.0 copy-done.2
  172.2 0.7 multiply_subtract_fusion.1
  173.0 0.0 copy-start.1
  173.0 0.0 all-gather.12.cloned.1.call-update
  173.0 0.0 all-gather.14.cloned.1.call-start
  173.0 27.9 %all-gather.12.cloned.1.call-done = f32[4096,128]{1,0:T(8,128)} async-done(((f32[512,128]{1,0:T(8,128)}), f32[4096,128]{1,0:T(8,128)}) %all-gather.12.cloned.1.call-update) | async-done | bytes 2097168 | tf_op jit(solution)/shard_map/all_gather | solution.py:38
  200.9 10.1 %multiply_reduce_fusion.3 = (f32[128]{0:T(128)S(1)}, f32[128]{0:T(128)S(1)}, f32[512,128]{1,0:T(8,128)S(1)}) fusion(f32[512,128]{1,0:T(8,128)} %multiply_subtract_fusion.1, f32[4096,128]{1,0:T(8,128)} %all-gather.12.cloned.1.call-done, f32[512,4096]{1,0:T(8,128)} %reduce_sum.109, s32[512]{0:T(512)S(1)} %iota_add_fusion), kind=kOutput, calls=%fused_computation.17 | convolution fusion | flops 3227778816 | bytes 11013120 | tf_op jit(solution)/shard_map/dot_general | solution.py:33
  211.1 13.3 %all-reduce.1 = (f32[128]{0:T(128)S(1)}, f32[128]{0:T(128)S(1)}) all-reduce(f32[128]{0:T(128)S(1)} %get-tuple-element.5, f32[128]{0:T(128)S(1)} %get-tuple-element.4), channel_id=1, replica_groups=mesh['grp'=4,'row'=8] {'row'}, use_global_device_ids=true, to_apply=%region_10.0 | all-reduce | flops 256 | bytes 2048 | tf_op jit(solution)/shard_map/psum | solution.py:10
  224.4 0.0 copy-done.1
  224.4 0.8 multiply_subtract_fusion
  225.2 0.0 copy-start.3
  225.2 0.0 all-gather.14.cloned.1.call-update
  225.2 27.9 %all-gather.14.cloned.1.call-done = f32[4096,128]{1,0:T(8,128)} async-done(((f32[512,128]{1,0:T(8,128)}), f32[4096,128]{1,0:T(8,128)}) %all-gather.14.cloned.1.call-update) | async-done | bytes 2097168 | tf_op jit(solution)/shard_map/all_gather | solution.py:38
  253.1 10.1 %multiply_reduce_fusion.1 = (f32[128]{0:T(128)S(1)}, f32[128]{0:T(128)S(1)}, f32[512,128]{1,0:T(8,128)S(1)}) fusion(f32[512,128]{1,0:T(8,128)} %get-tuple-element.22, f32[4096,128]{1,0:T(8,128)} %all-gather.14.cloned.1.call-done, f32[512,4096]{1,0:T(8,128)} %reduce_sum.109, s32[512]{0:T(512)S(1)} %iota_add_fusion), kind=kOutput, calls=%fused_computation.13 | convolution fusion | flops 3227778816 | bytes 11013120 | tf_op jit(solution)/shard_map/dot_general | solution.py:33
  263.3 13.1 %all-reduce = (f32[128]{0:T(128)S(1)}, f32[128]{0:T(128)S(1)}) all-reduce(f32[128]{0:T(128)S(1)} %get-tuple-element.3, f32[128]{0:T(128)S(1)} %get-tuple-element.2), channel_id=1, replica_groups=mesh['grp'=4,'row'=8] {'row'}, use_global_device_ids=true, to_apply=%region_14.0 | all-reduce | flops 256 | bytes 2048 | tf_op jit(solution)/shard_map/psum | solution.py:10
  276.4 0.0 copy-done.3
  276.4 0.9 multiply_reduce_fusion
  277.3 11.8 %psum.85 = f32[128]{0:T(128)S(1)} all-reduce(f32[128]{0:T(128)S(1)} %get-tuple-element.30), channel_id=1, replica_groups=mesh['grp'=4,'row'=8] {'row'}, use_global_device_ids=true, to_apply=%region_18.0 | all-reduce | flops 128 | bytes 1024 | tf_op jit(solution)/shard_map/psum | solution.py:59
  289.0 0.7 reduce_sum.118
  289.7 12.4 %all-reduce.4 = (f32[]{:T(128)}, f32[]{:T(128)}) all-reduce(f32[]{:T(128)} %reduce_sum.118, f32[]{:T(128)} %get-tuple-element.32), channel_id=1, replica_groups=mesh['grp'=4,'row'=8] {'grp'}, use_global_device_ids=true, to_apply=%region_20.0 | all-reduce | flops 2 | bytes 16 | tf_op jit(solution)/shard_map/psum | solution.py:60
  (4 shorter events, 0.0 us)
Async XLA Ops:
  7.2 42.1 %all-gather.6.cloned.1.call-start = ((), (), s32[]{:S(2)}) async-start(), calls=%async_computation | async-start | bytes 4718592 | tf_op jit(solution)/shard_map/all_gather | solution.py:27
  7.9 88.6 %all-gather.8.cloned.1.call-start = ((), (), s32[]{:S(2)}) async-start(), calls=%async_computation.1 | async-start | bytes 2359296 | tf_op jit(solution)/shard_map/all_gather | solution.py:38
  68.6 79.8 %all-gather.10.cloned.1.call-start = ((), (), s32[]{:S(2)}) async-start(), calls=%async_computation.2 | async-start | bytes 2359296 | tf_op jit(solution)/shard_map/all_gather | solution.py:38
  68.6 27.9 %copy-start = (f32[512,128]{1,0:T(8,128)S(1)}, f32[512,128]{1,0:T(8,128)}, u32[]{:S(2)}) copy-start(f32[512,128]{1,0:T(8,128)} %convolution_bitcast_fusion) | copy-start | bytes 786436
  120.4 51.8 %copy-start.2 = (f32[512,128]{1,0:T(8,128)S(1)}, f32[512,128]{1,0:T(8,128)}, u32[]{:S(2)}) copy-start(f32[512,128]{1,0:T(8,128)} %multiply_subtract_fusion.2) | copy-start | bytes 786436
  120.5 80.5 %all-gather.12.cloned.1.call-start = ((), (), s32[]{:S(2)}) async-start(), calls=%async_computation.3 | async-start | bytes 2359296 | tf_op jit(solution)/shard_map/all_gather | solution.py:38
  173.0 51.4 %copy-start.1 = (f32[512,128]{1,0:T(8,128)S(1)}, f32[512,128]{1,0:T(8,128)}, u32[]{:S(2)}) copy-start(f32[512,128]{1,0:T(8,128)} %multiply_subtract_fusion.1) | copy-start | bytes 786436
  173.0 80.1 %all-gather.14.cloned.1.call-start = ((), (), s32[]{:S(2)}) async-start(), calls=%async_computation.4 | async-start | bytes 2359296 | tf_op jit(solution)/shard_map/all_gather | solution.py:38
  225.2 51.2 %copy-start.3 = (f32[512,128]{1,0:T(8,128)S(1)}, f32[512,128]{1,0:T(8,128)}, u32[]{:S(2)}) copy-start(f32[512,128]{1,0:T(8,128)} %get-tuple-element.22) | copy-start | bytes 786436
Sparse Core Ops, SparseCore 0:
  9.9 39.2 all-gather.5
  68.7 27.7 all-gather.7
  120.6 27.7 all-gather.9
  173.1 27.7 all-gather.11
  225.3 27.7 all-gather.13
where the time goes:
time: 311 us
  waiting for transfers between devices  138 us (44%)
  blocking collectives  76.7 us (25%)
  matrix products  59.8 us (19%)
  other arithmetic  20.3 us (7%)
  between operations  16.4 us (5%)
    all_gather x4, waiting for transfers between devices, apply_system(): return add_panel(lax.all_gather(vectors, 'row', axis=0, tiled=True))  95.6 us
    psum x4, blocking collectives, both_sums(): lax.psum((jnp.sum(residual * residual, axis=0), jnp.sum(residual * mapped...  52.6 us
    all_gather x1, waiting for transfers between devices, local(): lax.all_gather(expert_weights, 'row', axis=1, tiled=True)  41.3 us
    dot_general x4, matrix products, add_panel(): jnp.dot(system, incoming, precision=lax.Precision.HIGHEST, preferred_elem...  40.5 us
    dot_general x1, matrix products, local(): jnp.einsum('krn,knc->rc', expert_grams, lax.all_gather(expert_weights, 'r...  19.3 us
    reduce_sum x1, other arithmetic, local(): jnp.sum(expert_grams, axis=0) + (row_ids == col_ids).astype(jnp.float32)  15.8 us
    psum x1, blocking collectives, local(): totals = lax.psum((jnp.sum(final_sums), jnp.sum(initial)), 'grp')  12.4 us
    psum x1, blocking collectives, local(): final_sums = lax.psum(jnp.sum(residual * residual, axis=0), 'row')  11.8 us
  transfers between devices with their start and end apart: 5, of which 5 were waited for; matrix products, arithmetic and copies ran while one was open for 5% of the time, Pallas kernels for 0%

commit v1 on v0

v1 whole, which is shorter than its diff:
```python
import functools

import jax
import jax.numpy as jnp
from jax import lax
from jax.experimental import pallas as pl
from jax.experimental.pallas import tpu as pltpu
from jax.sharding import PartitionSpec as P

ITERS = 4
SLOTS = 3
F32 = jnp.float32
BF16 = jnp.bfloat16


def split(x):
    high = x.astype(BF16)
    return high, (x - high.astype(F32)).astype(BF16)


def grid_side(chips):
    side = int(chips**0.5)
    while chips % side:
        side -= 1
    return chips // side


def kernel(
    n, groups,
    grams, weights, merged, ratio,
    panel, planes, wide, system, blocks, last_blocks,
    to_sibling, from_sibling, to_chip, from_chip,
    dots, totals, res, mapped, mapped_dir, second_dir, direction, second,
    gram_sem, sib_send, sib_recv, chip_send, chip_recv,
    block_send, block_recv, relay_send, dot_send, dot_recv, total_send, total_recv,
):
    experts, rows, columns = weights.shape
    chips = n // 2
    side = grid_side(chips)
    me = lax.axis_index("row")
    group = lax.axis_index("grp")
    core = lax.rem(me, 2)
    chip = me // 2
    sibling = chip * 2 + 1 - core

    def chip_at(t):
        up = lax.rem(chip // side + t // side, chips // side)
        return up * side + lax.rem(lax.rem(chip, side) + lax.rem(t, side), side)

    def chip_from(t):
        down = lax.rem(chip // side + chips // side - t // side, chips // side)
        return down * side + lax.rem(lax.rem(chip, side) + side - lax.rem(t, side), side)

    def chunk_of(c):
        t = chips - 1 - c // 2
        half = lax.rem(c, 2)
        owner = jnp.where(half == 0, 1 - core, core)
        return chip_at(t) * 2 + owner

    def gram_copy(c):
        start = pl.multiple_of(chunk_of(c) * rows, rows)
        slot = lax.rem(c, SLOTS)
        return pltpu.make_async_copy(
            grams.at[:, :, pl.ds(start, rows)], panel.at[slot], gram_sem.at[slot]
        )

    for c in range(SLOTS - 1):
        gram_copy(jnp.int32(c)).start()

    barrier = pltpu.get_barrier_semaphore()
    for other in range(1, n):
        pl.semaphore_signal(
            barrier, inc=1, device_id={"row": lax.rem(me + other, n)},
            device_id_type=pl.DeviceIdType.MESH,
        )
    for other in range(1, groups):
        pl.semaphore_signal(
            barrier, inc=1, device_id={"grp": lax.rem(group + other, groups)},
            device_id_type=pl.DeviceIdType.MESH,
        )

    for expert in range(experts):
        turned = weights[expert].astype(F32).T.astype(BF16)
        wide[:, expert * rows : (expert + 1) * rows] = turned
        wide[:, (experts + expert) * rows : (experts + expert + 1) * rows] = turned

    pl.semaphore_wait(barrier, n - 1 + groups - 1)

    def send(src, dst, send_sem, recv_sem, axis, index):
        return pltpu.make_async_remote_copy(
            src_ref=src, dst_ref=dst, send_sem=send_sem, recv_sem=recv_sem,
            device_id={axis: index}, device_id_type=pl.DeviceIdType.MESH,
        )

    def sibling_copy(t):
        return send(
            to_sibling.at[t], from_sibling.at[t], sib_send.at[t], sib_recv.at[t], "row", sibling
        )

    def chip_copy(t):
        return send(
            to_chip.at[t], from_chip.at[t], chip_send.at[t], chip_recv.at[t],
            "row", chip_at(t) * 2 + core,
        )

    def absorb(c):
        gram_copy(c).wait()

        @pl.when(c + SLOTS - 1 < n)
        def _():
            gram_copy(c + SLOTS - 1).start()

        slot = lax.rem(c, SLOTS)
        at = chunk_of(c)
        tile = min(64, rows)

        def fill(i, carry):
            top = pl.multiple_of(i * tile, tile)
            total = jnp.zeros((tile, rows), F32)
            for expert in range(experts):
                part = panel[slot, expert, pl.ds(top, tile), :]
                total = total + part
                high, low = split(part)
                planes[pl.ds(expert * rows + top, tile), :] = high
                planes[pl.ds((experts + expert) * rows + top, tile), :] = low
            row_ids = me * rows + top + lax.broadcasted_iota(jnp.int32, (tile, rows), 0)
            col_ids = at * rows + lax.broadcasted_iota(jnp.int32, (tile, rows), 1)
            total = total + jnp.where(row_ids == col_ids, 1.0, 0.0)
            high, low = split(total)
            system[at, pl.ds(top, tile), :] = high
            system[at, pl.ds(rows + top, tile), :] = low
            return carry

        lax.fori_loop(0, rows // tile, fill, 0)
        return jnp.dot(wide[...], planes[...], preferred_element_type=F32).T

    def pair(i, carry):
        t = chips - 1 - i
        to_sibling[t] = absorb(2 * i)
        sibling_copy(t).start()
        mine = absorb(2 * i + 1)
        sibling_copy(t).wait_recv()
        to_chip[t] = mine + from_sibling[t]

        @pl.when(t > 0)
        def _():
            chip_copy(t).start()

        return carry

    lax.fori_loop(0, chips, pair, 0)

    res[...] = to_chip[0]

    def collect(i, carry):
        t = chips - 1 - i
        chip_copy(t).wait_recv()
        res[...] += from_chip[t]
        return carry

    lax.fori_loop(0, chips - 1, collect, 0)

    def block_copy(k, t, source):
        return block_op(k, source, block_send.at[k, t], chip_at(t) * 2 + core)

    def block_op(k, source, send_sem, target):
        store = last_blocks if k == ITERS - 1 else blocks.at[k]
        return send(
            store.at[source], store.at[source], send_sem, block_recv.at[k, source], "row", target
        )

    def multiply(k, source):
        if k == ITERS - 1:
            second[...] += jnp.dot(
                system[source, :rows, :], last_blocks[source], preferred_element_type=F32
            )
        else:
            full = jnp.dot(system[source], blocks[k, source], preferred_element_type=F32)
            full = full[:rows] + full[rows:]
            second[...] += full[:, :columns] + full[:, columns:]

    def dot_copy(k, other):
        return send(
            dots.at[k, me], dots.at[k, me], dot_send.at[k, other], dot_recv.at[k, me],
            "row", lax.rem(me + other, n),
        )

    def dot_wait(k, other):
        source = lax.rem(me + other, n)
        return send(
            dots.at[k, source], dots.at[k, source], dot_send.at[k, other],
            dot_recv.at[k, source], "row", source,
        )

    def share(k, first, other=None):
        dots[k, me, 0:1, :] = first
        if other is not None:
            dots[k, me, 1:2, :] = other

        def go(o, carry):
            dot_copy(k, o).start()
            return carry

        lax.fori_loop(1, n, go, 0)

    def shared(k):
        def take(o, carry):
            dot_wait(k, o).wait_recv()
            return carry

        lax.fori_loop(1, n, take, 0)
        both = jnp.sum(dots[k], axis=0)
        return both[0:1, :], both[1:2, :]

    def column_sum(x):
        return jnp.sum(x, axis=0, keepdims=True)

    def spread(k, value):
        high, low = split(value)
        if k == ITERS - 1:
            last_blocks[me] = high
        else:
            blocks[k, me, :, :columns] = high
            blocks[k, me, :, columns:] = low
        block_op(k, me, relay_send.at[k, 0], sibling).start()

        def go(i, carry):
            block_copy(k, chips - 1 - i, me).start()
            return carry

        lax.fori_loop(0, chips - 1, go, 0)

    def product(k):
        second[...] = jnp.zeros_like(second)
        multiply(k, me)
        block_op(k, sibling, relay_send.at[k, 0], sibling).wait_recv()
        multiply(k, sibling)

        def take(t, carry):
            source = chip_from(t)
            near = source * 2 + core
            block_op(k, near, relay_send.at[k, t], sibling).wait_recv()
            block_op(k, near, relay_send.at[k, t], sibling).start()
            multiply(k, near)
            far = source * 2 + 1 - core
            block_op(k, far, relay_send.at[k, t], sibling).wait_recv()
            multiply(k, far)
            return carry

        lax.fori_loop(1, chips, take, 0)

    for k in range(ITERS + 1):
        dots[k, me] = jnp.zeros(dots.shape[2:], F32)

    spread(0, res[...])
    product(0)
    mapped[...] = second[...]
    mapped_dir[...] = jnp.zeros_like(mapped_dir)
    second_dir[...] = jnp.zeros_like(second_dir)
    direction[...] = jnp.zeros_like(direction)
    merged[...] = jnp.zeros_like(merged)

    initial = None
    norm_before = None
    step_before = None
    for k in range(ITERS):
        more = k + 1 < ITERS
        if more:
            spread(k + 1, mapped[...])
        share(k, column_sum(res[...] * res[...]), column_sum(res[...] * mapped[...]))
        if more:
            product(k + 1)
        norm, along = shared(k)
        if k == 0:
            initial = norm
            step = norm / along
            scaling = jnp.zeros_like(norm)
        else:
            scaling = norm / norm_before
            step = norm / (along - scaling * norm / step_before)
        norm_before, step_before = norm, step
        ahead = res[...] + scaling * direction[...]
        direction[...] = ahead
        merged[...] += step * ahead
        ahead = mapped[...] + scaling * mapped_dir[...]
        mapped_dir[...] = ahead
        res[...] -= step * ahead
        if more:
            ahead = second[...] + scaling * second_dir[...]
            second_dir[...] = ahead
            mapped[...] -= step * ahead

    share(ITERS, column_sum(res[...] * res[...]))
    final, _ = shared(ITERS)

    def total_copy(other):
        return send(
            totals.at[group], totals.at[group], total_send.at[other], total_recv.at[group],
            "grp", lax.rem(group + other, groups),
        )

    totals[group] = jnp.zeros(totals.shape[1:], F32)
    totals[group, 0:1, :] = final
    totals[group, 1:2, :] = initial
    for other in range(1, groups):
        total_copy(other).start()
    for other in range(1, groups):
        source = lax.rem(group + other, groups)
        send(
            totals.at[source], totals.at[source], total_send.at[other], total_recv.at[source],
            "grp", source,
        ).wait_recv()
    both = jnp.sum(jnp.sum(totals[...], axis=0), axis=1, keepdims=True)
    ratio[...] = jnp.broadcast_to(jnp.sqrt(both[0:1] / both[1:2]), ratio.shape)

    for other in range(1, groups):
        total_copy(other).wait_send()
    for k in range(ITERS + 1):
        def drain_dots(o, carry):
            dot_copy(k, o).wait_send()
            return carry

        lax.fori_loop(1, n, drain_dots, 0)
    for k in range(ITERS):
        block_op(k, me, relay_send.at[k, 0], sibling).wait_send()

        def drain_blocks(t, carry):
            block_copy(k, t, me).wait_send()
            block_op(k, me, relay_send.at[k, t], sibling).wait_send()
            return carry

        lax.fori_loop(1, chips, drain_blocks, 0)

    def drain_sums(t, carry):
        sibling_copy(t).wait_send()

        @pl.when(t > 0)
        def _():
            chip_copy(t).wait_send()

        return carry

    lax.fori_loop(0, chips, drain_sums, 0)


def local(n, groups, expert_grams, expert_weights):
    experts, rows, width = expert_grams.shape
    columns = expert_weights.shape[2]
    chips = n // 2
    vector = pltpu.VMEM((rows, columns), F32)
    dma = pltpu.SemaphoreType.DMA
    merged, ratio = pl.pallas_call(
        functools.partial(kernel, n, groups),
        out_shape=(
            jax.ShapeDtypeStruct((rows, columns), F32),
            jax.ShapeDtypeStruct((8, 128), F32),
        ),
        in_specs=[
            pl.BlockSpec(memory_space=pl.ANY),
            pl.BlockSpec(memory_space=pltpu.VMEM),
        ],
        out_specs=(
            pl.BlockSpec(memory_space=pltpu.VMEM),
            pl.BlockSpec(memory_space=pltpu.VMEM),
        ),
        scratch_shapes=[
            pltpu.VMEM((SLOTS, experts, rows, rows), F32),
            pltpu.VMEM((2 * experts * rows, rows), BF16),
            pltpu.VMEM((columns, 2 * experts * rows), BF16),
            pltpu.VMEM((n, 2 * rows, rows), BF16),
            pltpu.VMEM((ITERS - 1, n, rows, 2 * columns), BF16),
            pltpu.VMEM((n, rows, columns), BF16),
            pltpu.VMEM((chips, rows, columns), F32),
            pltpu.VMEM((chips, rows, columns), F32),
            pltpu.VMEM((chips, rows, columns), F32),
            pltpu.VMEM((chips, rows, columns), F32),
            pltpu.VMEM((ITERS + 1, n, 8, columns), F32),
            pltpu.VMEM((groups, 8, columns), F32),
            vector, vector, vector, vector, vector, vector,
            dma((SLOTS,)),
            dma((chips,)), dma((chips,)), dma((chips,)), dma((chips,)),
            dma((ITERS, chips)), dma((ITERS, n)), dma((ITERS, chips)),
            dma((ITERS + 1, n)), dma((ITERS + 1, n)), dma((groups,)), dma((groups,)),
        ],
        compiler_params=pltpu.CompilerParams(
            collective_id=0, has_side_effects=True, vmem_limit_bytes=60 * 1024 * 1024
        ),
    )(expert_grams, expert_weights)
    return merged, ratio[0, 0]


def solution(mesh):
    placed = (P(None, "row", None), P(None, "row", "grp"))
    body = functools.partial(local, mesh.shape["row"], mesh.shape["grp"])
    return jax.shard_map(
        body, mesh=mesh, in_specs=placed, out_specs=(P("row", "grp"), P()), check_vma=False
    )
```

time: 311 us -> 112 us (0.36)
  waiting for transfers between devices: 138 us -> 0 us
  Pallas kernels: 0 us -> 108 us
  blocking collectives: 76.7 us -> 0 us
  matrix products: 59.8 us -> 0 us
  other arithmetic: 20.3 us -> 0 us
  between operations: 16.4 us -> 0.64 us
    all_gather x5 -> x0, waiting for transfers between devices: 137 us -> none  [the longest x4 95.6 us: apply_system(): return add_panel(lax.all_gather(vectors, 'row', axis=0, tiled=True))]
    pallas_call x0 -> x1, Pallas kernels: none -> 108 us  [local(): pl.pallas_call(functools.partial(kernel, n, groups), out_shape=(jax.Shape...]
    psum x6 -> x0, blocking collectives: 76.7 us -> none  [the longest x4 52.6 us: both_sums(): lax.psum((jnp.sum(residual * residual, axis=0), jnp.sum(residual * mapped...]
    dot_general x5 -> x0, matrix products: 59.8 us -> none  [the longest x4 40.5 us: add_panel(): jnp.dot(system, incoming, precision=lax.Precision.HIGHEST, preferred_elem...]
    reduce_sum x3 -> x0, other arithmetic: 17.4 us -> none  [the longest x1 15.8 us: local(): jnp.sum(expert_grams, axis=0) + (row_ids == col_ids).astype(jnp.float32)]
  transfers between devices with their start and end apart: 5 -> 0, of which waited for: 5 -> 0; matrix products, arithmetic and copies ran while one was open for 5% -> 0% of each run, Pallas kernels for 0% -> 0%
where the time goes in v1:
time: 112 us
  Pallas kernels  108 us (96%)
  local copies, waits for them, and re-layouts  2.86 us (3%)
    pallas_call x1, Pallas kernels, local(): pl.pallas_call(functools.partial(kernel, n, groups), out_shape=(jax.Shape...  108 us

profile of v1, /device:TPU:0, one launch (start us, length us, event | category | flops | bytes accessed | tf_op | source)
XLA Modules:
  0.0 111.6 jit_solution(7478992226548785196)
XLA Ops:
  0.6 108.1 %shard_map.41 = (f32[512,128]{1,0:T(8,128)}, f32[8,128]{1,0:T(8,128)}) custom-call(f32[4,512,4096]{2,1,0:T(8,128)} %grams.1, bf16[4,512,128]{2,1,0:T(8,128)(2,1)} %weights.1), custom_call_target="tpu_custom_call" | custom-call | tf_op jit(solution)/shard_map/pallas_call | solution.py:352
  108.7 1.2 %slice.3 = f32[1,1]{1,0:T(1,128)} slice(f32[8,128]{1,0:T(8,128)} %get-tuple-element.5), slice={[0:1], [0:1]} | slice | bytes 8 | tf_op jit(solution)/shard_map/slice | solution.py:389
  109.9 1.7 %copy.5 = f32[512,128]{1,0:T(8,128)} copy(f32[512,128]{1,0:T(8,128)} %get-tuple-element.8) | data formatting | bytes 524288

commit v2 on v1

--- a/solution.py
+++ b/solution.py
@@ -8,7 +8,7 @@
 from jax.sharding import PartitionSpec as P
 
 ITERS = 4
-SLOTS = 3
+SLOTS = 4
 F32 = jnp.float32
 BF16 = jnp.bfloat16
 
@@ -32,7 +32,7 @@
     to_sibling, from_sibling, to_chip, from_chip,
     dots, totals, res, mapped, mapped_dir, second_dir, direction, second,
     gram_sem, sib_send, sib_recv, chip_send, chip_recv,
-    block_send, block_recv, relay_send, dot_send, dot_recv, total_send, total_recv,
+    block_send, block_recv, relay_send, hop_send, dot_send, dot_recv, total_send, total_recv,
 ):
     experts, rows, columns = weights.shape
     chips = n // 2
@@ -52,10 +52,11 @@
         return down * side + lax.rem(lax.rem(chip, side) + side - lax.rem(t, side), side)
 
     def chunk_of(c):
-        t = chips - 1 - c // 2
-        half = lax.rem(c, 2)
-        owner = jnp.where(half == 0, 1 - core, core)
-        return chip_at(t) * 2 + owner
+        odd = lax.rem(c, 2) == 1
+        t = jnp.where(odd, chips - 1 - (c + 1) // 2, chips - c // 2)
+        t = jnp.where(c == 0, chips - 1, jnp.where(c == n - 1, 0, t))
+        ahead = jnp.logical_or(c == 0, jnp.logical_and(odd, c < n - 1))
+        return chip_at(t) * 2 + jnp.where(ahead, 1 - core, core)
 
     def gram_copy(c):
         start = pl.multiple_of(chunk_of(c) * rows, rows)
@@ -134,23 +135,27 @@
         lax.fori_loop(0, rows // tile, fill, 0)
         return jnp.dot(wide[...], planes[...], preferred_element_type=F32).T
 
+    def hand_over(c, t):
+        to_sibling[t] = absorb(c)
+        sibling_copy(t).start()
+
+    def combine(c, t):
+        mine = absorb(c)
+        sibling_copy(t).wait_recv()
+        return mine + from_sibling[t]
+
+    hand_over(jnp.int32(0), chips - 1)
+
     def pair(i, carry):
+        hand_over(2 * i + 1, chips - 2 - i)
         t = chips - 1 - i
-        to_sibling[t] = absorb(2 * i)
-        sibling_copy(t).start()
-        mine = absorb(2 * i + 1)
-        sibling_copy(t).wait_recv()
-        to_chip[t] = mine + from_sibling[t]
-
-        @pl.when(t > 0)
-        def _():
-            chip_copy(t).start()
-
+        to_chip[t] = combine(2 * i + 2, t)
+        chip_copy(t).start()
         return carry
 
-    lax.fori_loop(0, chips, pair, 0)
-
-    res[...] = to_chip[0]
+    lax.fori_loop(0, chips - 1, pair, 0)
+
+    res[...] = combine(jnp.int32(n - 1), 0)
 
     def collect(i, carry):
         t = chips - 1 - i
@@ -160,14 +165,19 @@
 
     lax.fori_loop(0, chips - 1, collect, 0)
 
-    def block_copy(k, t, source):
-        return block_op(k, source, block_send.at[k, t], chip_at(t) * 2 + core)
-
-    def block_op(k, source, send_sem, target):
+    half = rows // 2
+    relayed = chips == 4 and side == 2
+
+    def block_op(k, source, h, send_sem, target):
         store = last_blocks if k == ITERS - 1 else blocks.at[k]
-        return send(
-            store.at[source], store.at[source], send_sem, block_recv.at[k, source], "row", target
-        )
+        piece = store.at[source, h * half : (h + 1) * half]
+        return send(piece, piece, send_sem, block_recv.at[k, source, h], "row", target)
+
+    def to_far(k, t, h):
+        return block_op(k, me, h, block_send.at[k, t, h], chip_at(t) * 2 + core)
+
+    def to_near(k, t, h, source):
+        return block_op(k, source, h, relay_send.at[k, t, h], sibling)
 
     def multiply(k, source):
         if k == ITERS - 1:
@@ -209,8 +219,8 @@
             return carry
 
         lax.fori_loop(1, n, take, 0)
-        both = jnp.sum(dots[k], axis=0)
-        return both[0:1, :], both[1:2, :]
+        sums = jnp.sum(dots[k], axis=0)
+        return sums[0:1, :], sums[1:2, :]
 
     def column_sum(x):
         return jnp.sum(x, axis=0, keepdims=True)
@@ -222,32 +232,79 @@
         else:
             blocks[k, me, :, :columns] = high
             blocks[k, me, :, columns:] = low
-        block_op(k, me, relay_send.at[k, 0], sibling).start()
+        if relayed:
+            for t, h in ((1, 0), (2, 1)):
+                to_far(k, t, h).start()
+            for h in (0, 1):
+                to_near(k, 0, h, me).start()
+            for t, h in ((1, 1), (2, 0)):
+                to_far(k, t, h).start()
+            return
+        for h in (0, 1):
+            to_near(k, 0, h, me).start()
 
         def go(i, carry):
-            block_copy(k, chips - 1 - i, me).start()
+            for h in (0, 1):
+                to_far(k, chips - 1 - i, h).start()
             return carry
 
         lax.fori_loop(0, chips - 1, go, 0)
+
+    def both(k, first, other):
+        def one(i, carry):
+            multiply(k, jnp.where(i == 0, first, other))
+            return carry
+
+        lax.fori_loop(0, 2, one, 0)
+
+    def arrive(k, source, h):
+        to_near(k, 0, h, source).wait_recv()
+
+    def hop(k, h, source):
+        return block_op(k, source, h, hop_send.at[k, h], chip_at(2 - h) * 2 + core)
 
     def product(k):
         second[...] = jnp.zeros_like(second)
-        multiply(k, me)
-        block_op(k, sibling, relay_send.at[k, 0], sibling).wait_recv()
-        multiply(k, sibling)
-
-        def take(t, carry):
-            source = chip_from(t)
-            near = source * 2 + core
-            block_op(k, near, relay_send.at[k, t], sibling).wait_recv()
-            block_op(k, near, relay_send.at[k, t], sibling).start()
+        for h in (0, 1):
+            arrive(k, sibling, h)
+        both(k, me, sibling)
+        if relayed:
+            by_x, by_y, by_both = (chip_at(t) * 2 for t in (1, 2, 3))
+            for t, h, source in ((1, 0, by_x), (2, 1, by_y)):
+                arrive(k, source + core, h)
+                hop(k, h, source + core).start()
+                to_near(k, t, h, source + core).start()
+            for t, h, source in ((1, 1, by_x), (2, 0, by_y)):
+                arrive(k, source + core, h)
+                to_near(k, t, h, source + core).start()
+            both(k, by_x + core, by_y + core)
+            for source in (by_x, by_y):
+                for h in (0, 1):
+                    arrive(k, source + 1 - core, h)
+            both(k, by_x + 1 - core, by_y + 1 - core)
+            for h in (0, 1):
+                arrive(k, by_both + core, h)
+                to_near(k, 3, h, by_both + core).start()
+            multiply(k, by_both + core)
+            for h in (0, 1):
+                arrive(k, by_both + 1 - core, h)
+            multiply(k, by_both + 1 - core)
+            return
+
+        def take(i, carry):
+            t = chips - 1 - i
+            near = chip_from(t) * 2 + core
+            for h in (0, 1):
+                arrive(k, near, h)
+                to_near(k, t, h, near).start()
             multiply(k, near)
-            far = source * 2 + 1 - core
-            block_op(k, far, relay_send.at[k, t], sibling).wait_recv()
+            far = chip_from(t) * 2 + 1 - core
+            for h in (0, 1):
+                arrive(k, far, h)
             multiply(k, far)
             return carry
 
-        lax.fori_loop(1, chips, take, 0)
+        lax.fori_loop(0, chips - 1, take, 0)
 
     for k in range(ITERS + 1):
         dots[k, me] = jnp.zeros(dots.shape[2:], F32)
@@ -310,8 +367,8 @@
             totals.at[source], totals.at[source], total_send.at[other], total_recv.at[source],
             "grp", source,
         ).wait_recv()
-    both = jnp.sum(jnp.sum(totals[...], axis=0), axis=1, keepdims=True)
-    ratio[...] = jnp.broadcast_to(jnp.sqrt(both[0:1] / both[1:2]), ratio.shape)
+    sums = jnp.sum(jnp.sum(totals[...], axis=0), axis=1, keepdims=True)
+    ratio[...] = jnp.broadcast_to(jnp.sqrt(sums[0:1] / sums[1:2]), ratio.shape)
 
     for other in range(1, groups):
         total_copy(other).wait_send()
@@ -322,14 +379,24 @@
 
         lax.fori_loop(1, n, drain_dots, 0)
     for k in range(ITERS):
-        block_op(k, me, relay_send.at[k, 0], sibling).wait_send()
-
-        def drain_blocks(t, carry):
-            block_copy(k, t, me).wait_send()
-            block_op(k, me, relay_send.at[k, t], sibling).wait_send()
-            return carry
-
-        lax.fori_loop(1, chips, drain_blocks, 0)
+        for h in (0, 1):
+            to_near(k, 0, h, me).wait_send()
+            if relayed:
+                hop(k, h, me).wait_send()
+
+        def drain_near(t, carry):
+            for h in (0, 1):
+                to_near(k, t, h, me).wait_send()
+            return carry
+
+        lax.fori_loop(1, chips, drain_near, 0)
+
+        def drain_far(t, carry):
+            for h in (0, 1):
+                to_far(k, t, h).wait_send()
+            return carry
+
+        lax.fori_loop(1, chips - 1 if relayed else chips, drain_far, 0)
 
     def drain_sums(t, carry):
         sibling_copy(t).wait_send()
@@ -379,7 +446,7 @@
             vector, vector, vector, vector, vector, vector,
             dma((SLOTS,)),
             dma((chips,)), dma((chips,)), dma((chips,)), dma((chips,)),
-            dma((ITERS, chips)), dma((ITERS, n)), dma((ITERS, chips)),
+            dma((ITERS, chips, 2)), dma((ITERS, n, 2)), dma((ITERS, chips, 2)), dma((ITERS, 2)),
             dma((ITERS + 1, n)), dma((ITERS + 1, n)), dma((groups,)), dma((groups,)),
         ],
         compiler_params=pltpu.CompilerParams(

time: 112 us -> 91.1 us (0.81)
  Pallas kernels: 108 us -> 87.4 us
    pallas_call x1, Pallas kernels: 108 us -> 87.4 us  [local(): pl.pallas_call(functools.partial(kernel, n, groups), out_shape=(jax.Shape...]
where the time goes in v2:
time: 91.1 us; the launch traced here: 90.9 us
  Pallas kernels  87.4 us (96%)
  local copies, waits for them, and re-layouts  2.86 us (3%)
    pallas_call x1, Pallas kernels, local(): pl.pallas_call(functools.partial(kernel, n, groups), out_shape=(jax.Shape...  87.4 us

profile of v2, /device:TPU:0, one launch (start us, length us, event | category | flops | bytes accessed | tf_op | source)
XLA Modules:
  0.0 90.9 jit_solution(9024410622246731332)
XLA Ops:
  0.6 87.4 %shard_map.41 = (f32[512,128]{1,0:T(8,128)}, f32[8,128]{1,0:T(8,128)}) custom-call(f32[4,512,4096]{2,1,0:T(8,128)} %grams.1, bf16[4,512,128]{2,1,0:T(8,128)(2,1)} %weights.1), custom_call_target="tpu_custom_call" | custom-call | tf_op jit(solution)/shard_map/pallas_call | solution.py:419
  88.0 1.2 %slice.3 = f32[1,1]{1,0:T(1,128)} slice(f32[8,128]{1,0:T(8,128)} %get-tuple-element.5), slice={[0:1], [0:1]} | slice | bytes 8 | tf_op jit(solution)/shard_map/slice | solution.py:456
  89.2 1.7 %copy.5 = f32[512,128]{1,0:T(8,128)} copy(f32[512,128]{1,0:T(8,128)} %get-tuple-element.8) | data formatting | bytes 524288
